TPU v7x, 256 devices: a whole 4x4x8 slice. The times are simulated.
256 devices in a mesh: member: 8 (over y_lo, x), grid: 32 (over z, y_hi, core).
Axes of the slice: x: 4, y: 4 (y_hi: 2, y_lo: 2; y = y_hi * 2 + y_lo), z: 8, core: 2. Of those that a mesh axis runs over, the one named last changes fastest.
Arguments:
- prior_ensemble: bfloat16 [40, 48, 131072], P('member', None, 'grid'), may hold values from -6 to 6
- domain_site_mapping: int32 [32, 8, 512], P(None, None, 'grid'), may hold values from 0 to 4095, as said below
- neighbour_triples: int32 [32, 3, 4096], P('grid', None, 'member'), may hold values from 0 to 159
- stencil_factors: float32 [32, 3, 4096], P('grid', None, 'member'), may hold values from 0.1 to 1
- sparse_node_transforms: float32 [1600, 4096], P(None, 'grid'), may hold values from -0.4 to 1.8
Outputs:
- analysis: bfloat16 [40, 48, 131072], P('member', None, 'grid')
Inputs may be any that keep to these rules, and one draw needn't show every extreme that they name: For every model patch h, the entries domain_site_mapping[:, :, h * 16 : (h + 1) * 16] hold every number from 0 to 4095 exactly once.
All inputs are finite; a program needn't handle non-finite values.
Results may differ from a plain program's by a relative error of at most 0.0076.
Values may be sent and summed in bfloat16 or wider, within the bound.
A program may use at most 128 MiB of HBM per device.

v0:
```python
import functools

import jax
import jax.numpy as jnp
from jax import lax
from jax.experimental import pallas as pl
from jax.experimental.pallas import tpu as pltpu
from jax.sharding import PartitionSpec as P

MESH = pl.DeviceIdType.MESH
F32, BF16 = jnp.float32, jnp.bfloat16

MEMBERS = 40
LOCAL = 5
FIELDS = 48
ROWS = LOCAL * FIELDS
PATCH = 4096
BLOCK = 512
GROUPS = 8
POINTS = 128
RIM = 16
PAIRS = 200
HEAD = 16
PACKET = HEAD + 208


def onehot_into(oh_ref, hi_ref, ids):
    hi, lo = ids >> 6, ids & 63
    level = lax.broadcasted_iota(jnp.int32, (64, BLOCK), 0)
    hi_ref[...] = jnp.where(level == hi, 1.0, 0.0).astype(F32)
    low = jnp.where(level == lo, 1.0, 0.0).astype(BF16).reshape(4, 16, BLOCK)
    for h in range(64):
        row = jnp.broadcast_to(hi_ref[h : h + 1, :], (16, BLOCK)).astype(BF16)
        oh_ref[h * 64 : (h + 1) * 64, :] = (low * row[None]).reshape(64, BLOCK)


def kernel(
    prior_ref, ids_ref, pts_ref, fac_ref, trans_ref, out_ref,
    zsend, zrecv, tbuf, rimsend, rimbuf, picked, gathered, mean, dev, weights,
    result, returned, total, oh, hi_ref, spread, spread_rim,
    zs_send, zs_recv, t_send, t_recv, d_sems, rim_send, rim_recv,
    st_send, st_recv, rt_send, rt_recv,
):
    m, g = lax.axis_index("member"), lax.axis_index("grid")
    z, q = g // 4, g % 4
    yh, c = q // 2, q % 2
    rim_end = jnp.logical_or(q == 0, q == 3)
    low_end = q == 3
    rim_member = jnp.where(low_end, (z + 1) % 8, (z + 7) % 8)

    barrier = pltpu.get_barrier_semaphore()

    def greet(member, grid):
        pl.semaphore_signal(barrier, inc=1, device_id=(member, grid), device_id_type=MESH)

    for s in range(1, 8):
        greet(m, ((z + s) % 8) * 4 + q)
    for s in range(8):
        for other in range(2):
            if s or other:
                greet((m + s) % 8, z * 4 + ((yh + other) % 2) * 2 + c)
    greet(m, z * 4 + yh * 2 + (1 - c))
    greet(z, ((m + 7) % 8) * 4 + 3)
    greet(z, ((m + 1) % 8) * 4)

    @pl.when(rim_end)
    def _():
        for p in range(4):
            greet(rim_member, m * 4 + p)

    start = pl.multiple_of(m * PAIRS, 8)
    part = trans_ref[pl.ds(start, PAIRS), :].astype(BF16)
    raw = fac_ref[...]
    shares = raw / jnp.sum(raw, axis=0, keepdims=True)
    head = jnp.concatenate(
        [pts_ref[...].astype(F32), shares, jnp.zeros((HEAD - 6, BLOCK), F32)], axis=0
    ).astype(BF16)
    for j in range(4):
        zsend[j, 0:HEAD, :] = head[:, j * 128 : (j + 1) * 128]
        zsend[j, HEAD : HEAD + PAIRS, :] = part
        zsend[j, HEAD + PAIRS : PACKET, :] = jnp.zeros((8, POINTS), BF16)
    lane = lax.broadcasted_iota(jnp.int32, (PAIRS, POINTS), 1)
    packed = jnp.zeros((PAIRS, POINTS), F32)
    base = jnp.where(low_end, POINTS - RIM, 0)
    for b in range(8):
        block = trans_ref[b * PAIRS : (b + 1) * PAIRS, :]
        block = pltpu.roll(block, (b * RIM - base + POINTS) % POINTS, axis=1)
        packed = jnp.where(lane // RIM == b, block, packed)
    rimsend[0:PAIRS, :] = packed.astype(BF16)
    rimsend[PAIRS:208, :] = jnp.zeros((8, POINTS), BF16)

    pl.semaphore_wait(barrier, jnp.where(rim_end, 29, 25))

    def copy(src, dst, send, recv, member, grid):
        return pltpu.make_async_remote_copy(
            src_ref=src, dst_ref=dst, send_sem=send, recv_sem=recv,
            device_id=(member, grid), device_id_type=MESH,
        )

    def z_copy(s):
        to = (z + s) % 8
        return copy(zsend.at[to // 2], zrecv.at[z], zs_send.at[s], zs_recv.at[z], m, to * 4 + q)

    def rim_copy(p):
        which = jnp.where(low_end, 0, 1)
        return copy(
            rimsend, rimbuf.at[which], rim_send.at[p], rim_recv.at[which], rim_member, m * 4 + p
        )

    for s in range(1, 8):
        z_copy(s).start()

    @pl.when(rim_end)
    def _():
        for p in range(4):
            rim_copy(p).start()

    zrecv[z] = zsend[z // 2]

    def state_copy(to):
        return copy(
            picked.at[to], gathered.at[m], st_send.at[to], st_recv.at[m], to, g
        )

    def pick(s, carry):
        to = (m + s + 1) % 8
        onehot_into(oh, hi_ref, ids_ref[pl.ds(to, 1), :])
        chosen = jnp.dot(prior_ref[...], oh[...], preferred_element_type=F32).astype(BF16)

        @pl.when(s < 7)
        def _():
            picked[to] = chosen
            state_copy(to).start()

        @pl.when(s == 7)
        def _():
            gathered[m] = chosen

        return carry

    lax.fori_loop(0, 8, pick, 0)

    for s in range(1, 8):
        frm = (z + s) % 8
        copy(zsend.at[0], zrecv.at[frm], zs_send.at[s], zs_recv.at[frm], m, g).wait_recv()

    def plane_copy(s, other):
        to = (m + s) % 8
        side = (yh + other) % 2
        return copy(
            zrecv.at[to], tbuf.at[c, m, yh], t_send.at[s * 2 + other], t_recv.at[m * 2 + yh],
            to, z * 4 + side * 2 + c,
        )

    for s in range(8):
        for other in range(2):
            if s or other:
                plane_copy(s, other).start()
    tbuf[c, m, yh] = zrecv[m]

    for s in range(1, 8):
        frm = (m + s) % 8
        copy(picked.at[frm], gathered.at[frm], st_send.at[frm], st_recv.at[frm], frm, g).wait_recv()

    mean[...] = jnp.zeros((FIELDS, BLOCK), F32)

    def add_up(r, carry):
        part_sum = mean[...]
        for k in range(LOCAL):
            part_sum = part_sum + gathered[r, k * FIELDS : (k + 1) * FIELDS, :].astype(F32)
        mean[...] = part_sum
        return carry

    lax.fori_loop(0, GROUPS, add_up, 0)
    mean[...] = mean[...] / MEMBERS

    def deviate(r, carry):
        for k in range(LOCAL):
            x = gathered[r, k * FIELDS : (k + 1) * FIELDS, :].astype(F32)
            row = pl.multiple_of((r * LOCAL + k) * FIELDS, 8)
            dev[pl.ds(row, FIELDS), :] = (x - mean[...]).astype(BF16).astype(F32)
        return carry

    lax.fori_loop(0, GROUPS, deviate, 0)

    for s in range(8):
        for other in range(2):
            if s or other:
                frm, side = (m + s) % 8, (yh + other) % 2
                copy(
                    zrecv.at[frm], tbuf.at[c, frm, side], t_send.at[s * 2 + other],
                    t_recv.at[frm * 2 + side], frm, z * 4 + side * 2 + c,
                ).wait_recv()
    core_copy = copy(
        tbuf.at[c], tbuf.at[c], d_sems.at[0], d_sems.at[1], m, z * 4 + yh * 2 + (1 - c)
    )
    core_copy.start()
    copy(
        tbuf.at[1 - c], tbuf.at[1 - c], d_sems.at[0], d_sems.at[1], m, z * 4 + yh * 2 + (1 - c)
    ).wait_recv()
    copy(rimsend, rimbuf.at[0], rim_send.at[0], rim_recv.at[0], z, ((m + 7) % 8) * 4 + 3).wait_recv()
    copy(rimsend, rimbuf.at[1], rim_send.at[1], rim_recv.at[1], z, ((m + 1) % 8) * 4).wait_recv()

    offset = (z % 2) * 64 + q * 16
    lane16 = lax.broadcasted_iota(jnp.int32, (HEAD, POINTS), 1) // 16
    depth = lax.broadcasted_iota(jnp.int32, (BLOCK, POINTS), 0)
    params = []
    for p in range(4):
        gathered_head = jnp.zeros((HEAD, POINTS), F32)
        for r in range(8):
            tile = tbuf[p % 2, r, p // 2, 0:HEAD, :].astype(F32)
            tile = pltpu.roll(tile, (r * 16 - offset + POINTS) % POINTS, axis=1)
            gathered_head = jnp.where(lane16 == r, tile, gathered_head)
        params.append(gathered_head)
        column = jnp.zeros((BLOCK, POINTS), F32)
        for w in range(3):
            point = gathered_head[w : w + 1, :].astype(jnp.int32) + (p * POINTS - RIM)
            column = column + jnp.where(depth == point, gathered_head[w + 3 : w + 4, :], 0.0)
        spread[:, p * POINTS : (p + 1) * POINTS] = column.astype(BF16)

    rim_depth = lax.broadcasted_iota(jnp.int32, (POINTS, POINTS), 0)

    def blend(r, carry):
        shifted = rim_depth - r * RIM
        inside = rim_depth // RIM == r
        for end, p, back in ((0, 0, 0), (1, 3, POINTS + RIM)):
            column = jnp.zeros((POINTS, POINTS), F32)
            for w in range(3):
                point = params[p][w : w + 1, :].astype(jnp.int32) - back
                hit = jnp.logical_and(inside, shifted == point)
                column = column + jnp.where(hit, params[p][w + 3 : w + 4, :], 0.0)
            spread_rim[end] = column.astype(BF16)
        rows = jnp.concatenate(
            [tbuf[p % 2, r, p // 2, HEAD : HEAD + PAIRS, :] for p in range(4)], axis=1
        )
        main = jnp.dot(rows, spread[...], preferred_element_type=F32)
        lo = jnp.dot(rimbuf[0, 0:PAIRS, :], spread_rim[0], preferred_element_type=F32)
        hi = jnp.dot(rimbuf[1, 0:PAIRS, :], spread_rim[1], preferred_element_type=F32)
        whole = jnp.concatenate(
            [main[:, 0:128] + lo, main[:, 128:384], main[:, 384:512] + hi], axis=1
        )
        whole = whole.astype(BF16).astype(F32)
        for k in range(LOCAL):
            for to in range(GROUPS):
                row = k * MEMBERS + to * LOCAL
                weights[r * LOCAL + k, to, 0:LOCAL, :] = whole[row : row + LOCAL, :]
        return carry

    lax.fori_loop(0, GROUPS, blend, 0)

    def return_copy(to):
        return copy(result.at[to], returned.at[m], rt_send.at[to], rt_recv.at[m], to, g)

    def analyse(s, carry):
        to = (m + s + 1) % 8
        for b in range(4):
            lanes = slice(b * 128, (b + 1) * 128)

            def step(k, sums):
                x = dev[pl.ds(pl.multiple_of(k * FIELDS, 8), FIELDS), lanes]
                return tuple(
                    sums[j] + x * weights[k, to, j : j + 1, lanes] for j in range(LOCAL)
                )

            sums = lax.fori_loop(
                0, MEMBERS, step, tuple(jnp.zeros((FIELDS, 128), F32) for _ in range(LOCAL))
            )
            for j in range(LOCAL):
                value = (sums[j] + mean[:, lanes]).astype(BF16)

                @pl.when(s < 7)
                def _():
                    result[to, j * FIELDS : (j + 1) * FIELDS, lanes] = value

                @pl.when(s == 7)
                def _():
                    returned[m, j * FIELDS : (j + 1) * FIELDS, lanes] = value

        @pl.when(s < 7)
        def _():
            return_copy(to).start()

        return carry

    lax.fori_loop(0, 8, analyse, 0)

    total[...] = jnp.zeros((ROWS, PATCH), F32)

    def place(s, carry):
        frm = (m + 8 - s) % 8

        @pl.when(s > 0)
        def _():
            copy(
                result.at[frm], returned.at[frm], rt_send.at[frm], rt_recv.at[frm], frm, g
            ).wait_recv()

        onehot_into(oh, hi_ref, ids_ref[pl.ds(frm, 1), :])
        for b in range(8):
            cells = slice(b * 512, (b + 1) * 512)
            total[:, cells] += lax.dot_general(
                returned[frm], oh[cells, :], (((1,), (1,)), ((), ())), preferred_element_type=F32
            )
        return carry

    lax.fori_loop(0, 8, place, 0)
    out_ref[...] = total[...].astype(BF16)

    for s in range(1, 8):
        z_copy(s).wait_send()
        state_copy((m + s) % 8).wait_send()
        return_copy((m + s) % 8).wait_send()
    for s in range(8):
        for other in range(2):
            if s or other:
                plane_copy(s, other).wait_send()
    core_copy.wait_send()

    @pl.when(rim_end)
    def _():
        for p in range(4):
            rim_copy(p).wait_send()


def on_device(prior, mapping, triples, factors, transforms):
    ids = mapping.reshape(GROUPS, BLOCK)
    vmem = pl.BlockSpec(memory_space=pltpu.VMEM)
    dma = pltpu.SemaphoreType.DMA
    out = pl.pallas_call(
        kernel,
        out_shape=jax.ShapeDtypeStruct((ROWS, PATCH), BF16),
        in_specs=[vmem] * 5,
        out_specs=vmem,
        scratch_shapes=[
            pltpu.VMEM((4, PACKET, POINTS), BF16),
            pltpu.VMEM((8, PACKET, POINTS), BF16),
            pltpu.VMEM((2, 8, 2, PACKET, POINTS), BF16),
            pltpu.VMEM((208, POINTS), BF16),
            pltpu.VMEM((2, 208, POINTS), BF16),
            pltpu.VMEM((8, ROWS, BLOCK), BF16),
            pltpu.VMEM((8, ROWS, BLOCK), BF16),
            pltpu.VMEM((FIELDS, BLOCK), F32),
            pltpu.VMEM((MEMBERS * FIELDS, BLOCK), F32),
            pltpu.VMEM((MEMBERS, GROUPS, 8, BLOCK), F32),
            pltpu.VMEM((8, ROWS, BLOCK), BF16),
            pltpu.VMEM((8, ROWS, BLOCK), BF16),
            pltpu.VMEM((ROWS, PATCH), F32),
            pltpu.VMEM((PATCH, BLOCK), BF16),
            pltpu.VMEM((64, BLOCK), F32),
            pltpu.VMEM((BLOCK, BLOCK), BF16),
            pltpu.VMEM((2, POINTS, POINTS), BF16),
            dma((8,)), dma((8,)), dma((16,)), dma((16,)), dma((2,)), dma((4,)), dma((2,)),
            dma((8,)), dma((8,)), dma((8,)), dma((8,)),
        ],
        compiler_params=pltpu.CompilerParams(
            collective_id=0, has_side_effects=True, vmem_limit_bytes=62 * 1024 * 1024
        ),
    )(prior.reshape(ROWS, PATCH), ids, triples[0], factors[0], transforms)
    return out.reshape(LOCAL, FIELDS, PATCH)


def solution(mesh):
    return jax.shard_map(
        on_device,
        mesh=mesh,
        in_specs=(
            P("member", None, "grid"),
            P(None, None, "grid"),
            P("grid", None, "member"),
            P("grid", None, "member"),
            P(None, "grid"),
        ),
        out_specs=P("member", None, "grid"),
        check_vma=False,
    )
```

profile of v0, /device:TPU:65, one launch (start us, length us, event | category | flops | bytes accessed | tf_op | source)
XLA Modules:
  0.0 112.7 jit_solution(1110353992165994879)
XLA Ops:
  0.0 1.3 %copy.13 = s32[1,3,512]{2,1,0:T(4,128)} copy(s32[1,3,512]{2,0,1:T(1,128)} %param.7) | data formatting | bytes 12288
  1.3 1.3 %copy.12 = f32[1,3,512]{2,1,0:T(4,128)} copy(f32[1,3,512]{2,0,1:T(1,128)} %param.8) | data formatting | bytes 12288
  2.6 0.9 copy.7
  3.5 0.7 reshape.10.ids_ref
  4.2 105.4 %shard_map.55 = bf16[240,4096]{1,0:T(8,128)(2,1)} custom-call(bf16[240,4096]{1,0:T(8,128)(2,1)} %bitcast.9, s32[8,512]{1,0:T(8,128)} %reshape.10.ids_ref, s32[3,512]{1,0:T(4,128)} %bitcast.10, f32[3,512]{1,0:T(4,128)} %bitcast.11, f32[1600,128]{1,0:T(8,128)} %trans_ref.1), custom_call_target="tpu_custom_call" | custom-call | tf_op jit(solution)/shard_map/pallas_call | solution.py:329
  109.6 3.0 %copy.15 = bf16[5,48,4096]{2,1,0:T(8,128)(2,1)} copy(bf16[5,48,4096]{2,1,0:T(8,128)(2,1)} %bitcast.8) | data formatting | bytes 3932160
where the time goes:
time: 113 us
  Pallas kernels  105 us (93%)
  local copies, waits for them, and re-layouts  7.25 us (6%)
    pallas_call x1, Pallas kernels, on_device(): pl.pallas_call(kernel, out_shape=jax.ShapeDtypeStruct((ROWS, PATCH), BF16...  105 us
    unnamed x4, local copies, waits for them, and re-layouts  6.53 us

commit v1 on v0

v1 whole, which is shorter than its diff:
```python
import functools

import jax
import jax.numpy as jnp
from jax import lax
from jax.experimental import pallas as pl
from jax.experimental.pallas import tpu as pltpu
from jax.sharding import PartitionSpec as P

MESH = pl.DeviceIdType.MESH
F32, BF16 = jnp.float32, jnp.bfloat16

MEMBERS = 40
LOCAL = 5
FIELDS = 48
ROWS = LOCAL * FIELDS
PATCH = 4096
BLOCK = 512
GROUPS = 8
POINTS = 128
RIM = 16
PAIRS = 200
HEAD = 16


def onehot_into(oh_ref, hi_ref, ids):
    hi, lo = ids >> 6, ids & 63
    level = lax.broadcasted_iota(jnp.int32, (64, BLOCK), 0)
    hi_ref[...] = jnp.where(level == hi, 1.0, 0.0).astype(F32)
    low = jnp.where(level == lo, 1.0, 0.0).astype(BF16).reshape(4, 16, BLOCK)
    for h in range(64):
        row = jnp.broadcast_to(hi_ref[h : h + 1, :], (16, BLOCK)).astype(BF16)
        oh_ref[h * 64 : (h + 1) * 64, :] = (low * row[None]).reshape(64, BLOCK)


def kernel(
    prior_ref, map_ref, pts_ref, fac_ref, trans_ref, out_ref,
    ids_ref, zsend, zrecv, pbuf, tsend, tbuf, rimsend, rimbuf, picked, gathered, mean, dev,
    weights, result, returned, total, oh, hi_ref, params, spread, spread_rim,
    zs_send, zs_recv, p_send, p_recv, d_sems, rim_send, rim_recv, y_send, t_send, t_back,
    t_recv, c_send, c_recv, st_send, st_recv, rt_send, rt_recv,
):
    m, g = lax.axis_index("member"), lax.axis_index("grid")
    z, q = g // 4, g % 4
    yh, c = q // 2, q % 2
    rim_end = jnp.logical_or(q == 0, q == 3)
    low_end = q == 3
    rim_member = jnp.where(low_end, (z + 1) % 8, (z + 7) % 8)
    far = (z - m + 8) % 8
    root, tail = far == 0, far == 4
    passes_on = jnp.logical_and(far != 4, far != 5)
    ahead = jnp.where(far <= 3, (z + 1) % 8, (z + 7) % 8)
    near = jnp.logical_or(far == 1, far == 7)

    barrier = pltpu.get_barrier_semaphore()

    def greet(member, grid):
        pl.semaphore_signal(barrier, inc=1, device_id=(member, grid), device_id_type=MESH)

    for s in range(1, 8):
        greet(m, ((z + s) % 8) * 4 + q)
    for s in range(8):
        for other in range(2):
            if s or other:
                greet((m + s) % 8, z * 4 + ((yh + other) % 2) * 2 + c)
    greet(m, z * 4 + yh * 2 + (1 - c))
    greet(z, ((m + 7) % 8) * 4 + 3)
    greet(z, ((m + 1) % 8) * 4)

    @pl.when(rim_end)
    def _():
        for p in range(4):
            greet(rim_member, m * 4 + p)

    mapping = map_ref[...].reshape(GROUPS * 16, 32)
    mapping = jnp.concatenate([mapping, jnp.zeros((GROUPS * 16, 96), jnp.int32)], axis=1)
    mapping = jnp.transpose(mapping)
    for to in range(GROUPS):
        ids_ref[to] = mapping[to * 4 : (to + 1) * 4, :]

    def ids_of(to):
        return jnp.concatenate([ids_ref[to, p : p + 1, :] for p in range(4)], axis=1)

    raw = [fac_ref[w] for w in range(3)]
    raw_sum = raw[0] + raw[1] + raw[2]
    head = jnp.concatenate(
        [pts_ref[w].astype(F32) for w in range(3)]
        + [raw[w] / raw_sum for w in range(3)]
        + [jnp.zeros((HEAD - 6, BLOCK), F32)],
        axis=0,
    ).astype(BF16)
    for j in range(4):
        zsend[j] = head[:, j * 128 : (j + 1) * 128]
    lane = lax.broadcasted_iota(jnp.int32, (PAIRS, POINTS), 1)
    packed = jnp.zeros((PAIRS, POINTS), F32)
    base = jnp.where(low_end, POINTS - RIM, 0)
    for b in range(8):
        block = trans_ref[b * PAIRS : (b + 1) * PAIRS, :]
        tsend[b] = block.astype(BF16)

        @pl.when(root)
        def _():
            tbuf[c, b, yh] = trans_ref[b * PAIRS : (b + 1) * PAIRS, :].astype(BF16)

        block = pltpu.roll(block, (b * RIM - base + POINTS) % POINTS, axis=1)
        packed = jnp.where(lane // RIM == b, block, packed)
    rimsend[...] = packed.astype(BF16)

    pl.semaphore_wait(barrier, jnp.where(rim_end, 29, 25))

    def copy(src, dst, send, recv, member, grid):
        return pltpu.make_async_remote_copy(
            src_ref=src, dst_ref=dst, send_sem=send, recv_sem=recv,
            device_id=(member, grid), device_id_type=MESH,
        )

    def z_copy(s):
        to = (z + s) % 8
        return copy(zsend.at[to // 2], zrecv.at[z], zs_send.at[s], zs_recv.at[z], m, to * 4 + q)

    def rim_copy(p):
        which = jnp.where(low_end, 0, 1)
        return copy(
            rimsend, rimbuf.at[which], rim_send.at[p], rim_recv.at[which], rim_member, m * 4 + p
        )

    def y_copy(r):
        return copy(
            tsend.at[r], tbuf.at[c, r, yh], y_send.at[r], t_recv.at[yh * 8 + r],
            (m + 4) % 8, z * 4 + (1 - yh) * 2 + c,
        )

    def t_copy(r, side, sems, to):
        slot = side * 8 + r
        return copy(
            tbuf.at[c, r, side], tbuf.at[c, r, side], sems.at[slot], t_recv.at[slot],
            m, to * 4 + q,
        )

    def c_copy(core, r, side):
        slot = side * 8 + r
        return copy(
            tbuf.at[core, r, side], tbuf.at[core, r, side], c_send.at[slot], c_recv.at[slot],
            m, z * 4 + yh * 2 + (1 - c),
        )

    for s in range(1, 8):
        z_copy(s).start()

    @pl.when(tail)
    def _():
        for r in range(8):
            y_copy(r).start()

    @pl.when(rim_end)
    def _():
        for p in range(4):
            rim_copy(p).start()

    zrecv[z] = zsend[z // 2]

    def relay(r):
        for other in range(2):
            side = (yh + other) % 2
            if other:
                t_copy(r, side, t_send, ahead).wait_recv()
            else:

                @pl.when(jnp.logical_not(root))
                def _():
                    t_copy(r, side, t_send, ahead).wait_recv()

            @pl.when(passes_on)
            def _():
                t_copy(r, side, t_send, ahead).start()

            @pl.when(root)
            def _():
                t_copy(r, side, t_back, (z + 7) % 8).start()

            c_copy(c, r, side).start()

    def turn(s, sign):
        dx = jnp.where(
            jnp.logical_or(s == 0, s == 4), 1,
            jnp.where(
                jnp.logical_or(s == 2, s == 5), 3,
                jnp.where(jnp.logical_or(s == 3, s == 6), 2, 0),
            ),
        )
        dy = jnp.where(jnp.logical_or(s == 1, jnp.logical_and(s >= 4, s <= 6)), 1, 0)
        return ((m // 4 + dy) % 2) * 4 + (m % 4 + 4 + sign * dx) % 4

    def state_copy(to):
        return copy(picked.at[to], gathered.at[m], st_send.at[to], st_recv.at[m], to, g)

    def return_copy(to):
        return copy(result.at[to], returned.at[m], rt_send.at[to], rt_recv.at[m], to, g)

    def start_pieces(src, dst, send, recv, turns):
        for k in range(LOCAL):
            for t in turns:
                to = turn(t, 1)
                rows = pl.ds(k * FIELDS, FIELDS)
                copy(src.at[to, rows], dst.at[m, rows], send.at[to], recv.at[m], to, g).start()

    def param_copy(s, other):
        to = (m + s) % 8
        side = (yh + other) % 2
        return copy(
            zrecv.at[to], pbuf.at[c, m, yh], p_send.at[s * 2 + other], p_recv.at[m * 2 + yh],
            to, z * 4 + side * 2 + c,
        )

    def pick(s, carry):
        to = turn(s, 1)
        onehot_into(oh, hi_ref, ids_of(to))
        chosen = jnp.dot(prior_ref[...], oh[...], preferred_element_type=F32).astype(BF16)

        @pl.when(s < 7)
        def _():
            picked[to] = chosen

        @pl.when(s < 3)
        def _():
            state_copy(to).start()

        @pl.when(s == 6)
        def _():
            start_pieces(picked, gathered, st_send, st_recv, (3, 4, 5, 6))

        @pl.when(s == 7)
        def _():
            gathered[m] = chosen

        @pl.when(s == 2)
        def _():
            for t in range(1, 8):
                frm = (z + t) % 8
                copy(zsend.at[0], zrecv.at[frm], zs_send.at[t], zs_recv.at[frm], m, g).wait_recv()
            for t in range(8):
                for other in range(2):
                    if t or other:
                        param_copy(t, other).start()
            pbuf[c, m, yh] = zrecv[m]

        ready = jnp.logical_or(
            jnp.logical_and(root, s >= 2),
            jnp.logical_and(near, jnp.logical_or(s == 5, s == 7)),
        )

        @pl.when(ready)
        def _():
            relay(jnp.where(root, s - 2, (s - 5) // 2))

        return carry

    lax.fori_loop(0, 8, pick, 0)
    relayed = jnp.where(root, 6, jnp.where(near, 2, 0))

    for s in range(8):
        for other in range(2):
            if s or other:
                frm, side = (m + s) % 8, (yh + other) % 2
                copy(
                    zrecv.at[frm], pbuf.at[c, frm, side], p_send.at[s * 2 + other],
                    p_recv.at[frm * 2 + side], frm, z * 4 + side * 2 + c,
                ).wait_recv()
    core_copy = copy(
        pbuf.at[c], pbuf.at[c], d_sems.at[0], d_sems.at[1], m, z * 4 + yh * 2 + (1 - c)
    )
    core_copy.start()

    mean[...] = jnp.zeros((FIELDS, BLOCK), F32)

    def add_up(s):
        frm = turn(s, -1)

        @pl.when(s < 7)
        def _():
            copy(
                picked.at[frm], gathered.at[frm], st_send.at[frm], st_recv.at[frm], frm, g
            ).wait_recv()

        part_sum = mean[...]
        for k in range(LOCAL):
            part_sum = part_sum + gathered[frm, k * FIELDS : (k + 1) * FIELDS, :].astype(F32)
        mean[...] = part_sum

    def prepare():
        copy(
            pbuf.at[1 - c], pbuf.at[1 - c], d_sems.at[0], d_sems.at[1], m, z * 4 + yh * 2 + (1 - c)
        ).wait_recv()
        copy(
            rimsend, rimbuf.at[0], rim_send.at[0], rim_recv.at[0], z, ((m + 7) % 8) * 4 + 3
        ).wait_recv()
        copy(
            rimsend, rimbuf.at[1], rim_send.at[1], rim_recv.at[1], z, ((m + 1) % 8) * 4
        ).wait_recv()
        offset = (z % 2) * 64 + q * 16
        lane16 = lax.broadcasted_iota(jnp.int32, (HEAD, POINTS), 1) // 16
        depth = lax.broadcasted_iota(jnp.int32, (BLOCK, POINTS), 0)
        for p in range(4):
            in_order = jnp.zeros((HEAD, POINTS), F32)
            for r in range(8):
                tile = pbuf[p % 2, r, p // 2].astype(F32)
                tile = pltpu.roll(tile, (r * 16 - offset + POINTS) % POINTS, axis=1)
                in_order = jnp.where(lane16 == r, tile, in_order)
            params[p] = in_order
            column = jnp.zeros((BLOCK, POINTS), F32)
            for w in range(3):
                point = in_order[w : w + 1, :].astype(jnp.int32) + (p * POINTS - RIM)
                column = column + jnp.where(depth == point, in_order[w + 3 : w + 4, :], 0.0)
            spread[:, p * POINTS : (p + 1) * POINTS] = column.astype(BF16)

    rim_depth = lax.broadcasted_iota(jnp.int32, (POINTS, POINTS), 0)

    def blend(r):
        for side in range(2):
            c_copy(1 - c, r, side).wait_recv()
        shifted = rim_depth - r * RIM
        inside = rim_depth // RIM == r
        for end, p, back in ((0, 0, 0), (1, 3, POINTS + RIM)):
            column = jnp.zeros((POINTS, POINTS), F32)
            for w in range(3):
                point = params[p, w : w + 1, :].astype(jnp.int32) - back
                hit = jnp.logical_and(inside, shifted == point)
                column = column + jnp.where(hit, params[p, w + 3 : w + 4, :], 0.0)
            spread_rim[end] = column.astype(BF16)
        rows = jnp.concatenate([tbuf[p % 2, r, p // 2] for p in range(4)], axis=1)
        main = jnp.dot(rows, spread[...], preferred_element_type=F32)
        lo = jnp.dot(rimbuf[0], spread_rim[0], preferred_element_type=F32)
        hi = jnp.dot(rimbuf[1], spread_rim[1], preferred_element_type=F32)
        whole = jnp.concatenate(
            [main[:, 0:128] + lo, main[:, 128:384], main[:, 384:512] + hi], axis=1
        )
        whole = whole.astype(BF16).astype(F32)
        for k in range(LOCAL):
            for to in range(GROUPS):
                row = k * MEMBERS + to * LOCAL
                weights[r * LOCAL + k, to, 0:LOCAL, :] = whole[row : row + LOCAL, :]

    def arrive(r, carry):
        @pl.when(jnp.logical_and(r >= relayed, r < 8))
        def _():
            relay(r)

        @pl.when(r == 1)
        def _():
            prepare()

        @pl.when(r < 4)
        def _():
            add_up((r + 7) % 8)

        @pl.when(r >= 1)
        def _():
            blend(r - 1)

        return carry

    lax.fori_loop(0, 9, arrive, 0)

    def add_rest(s, carry):
        add_up(s)
        return carry

    lax.fori_loop(3, 7, add_rest, 0)
    mean[...] = mean[...] / MEMBERS

    def deviate(r, carry):
        for k in range(LOCAL):
            x = gathered[r, k * FIELDS : (k + 1) * FIELDS, :].astype(F32)
            row = pl.multiple_of((r * LOCAL + k) * FIELDS, 8)
            dev[pl.ds(row, FIELDS), :] = (x - mean[...]).astype(BF16).astype(F32)
        return carry

    lax.fori_loop(0, GROUPS, deviate, 0)

    def analyse(s, carry):
        to = turn(s, 1)
        for b in range(4):
            lanes = slice(b * 128, (b + 1) * 128)

            def step(i, sums):
                sums = list(sums)
                for k in range(8):
                    row = pl.multiple_of((i * 8 + k) * FIELDS, 8)
                    x = dev[pl.ds(row, FIELDS), lanes]
                    for j in range(LOCAL):
                        sums[j] = sums[j] + x * weights[i * 8 + k, to, j : j + 1, lanes]
                return tuple(sums)

            sums = lax.fori_loop(
                0, MEMBERS // 8, step, tuple(jnp.zeros((FIELDS, 128), F32) for _ in range(LOCAL))
            )
            for j in range(LOCAL):
                value = (sums[j] + mean[:, lanes]).astype(BF16)

                @pl.when(s < 7)
                def _():
                    result[to, j * FIELDS : (j + 1) * FIELDS, lanes] = value

                @pl.when(s == 7)
                def _():
                    returned[m, j * FIELDS : (j + 1) * FIELDS, lanes] = value

        @pl.when(s < 3)
        def _():
            return_copy(to).start()

        @pl.when(s == 4)
        def _():
            start_pieces(result, returned, rt_send, rt_recv, (3, 4))

        @pl.when(s == 6)
        def _():
            start_pieces(result, returned, rt_send, rt_recv, (5, 6))

        return carry

    lax.fori_loop(0, 8, analyse, 0)

    total[...] = jnp.zeros((ROWS, PATCH), F32)

    def place(i, carry):
        s = (i + 7) % 8
        frm = turn(s, -1)

        @pl.when(s < 7)
        def _():
            copy(
                result.at[frm], returned.at[frm], rt_send.at[frm], rt_recv.at[frm], frm, g
            ).wait_recv()

        onehot_into(oh, hi_ref, ids_of(frm))
        for b in range(8):
            cells = slice(b * 512, (b + 1) * 512)
            total[:, cells] += lax.dot_general(
                returned[frm], oh[cells, :], (((1,), (1,)), ((), ())), preferred_element_type=F32
            )
        return carry

    lax.fori_loop(0, 8, place, 0)
    out_ref[...] = total[...].astype(BF16)

    for s in range(1, 8):
        z_copy(s).wait_send()
        state_copy((m + s) % 8).wait_send()
        return_copy((m + s) % 8).wait_send()
    for s in range(8):
        for other in range(2):
            if s or other:
                param_copy(s, other).wait_send()
    core_copy.wait_send()
    for r in range(8):
        for side in range(2):
            c_copy(c, r, side).wait_send()

            @pl.when(passes_on)
            def _():
                t_copy(r, side, t_send, ahead).wait_send()

            @pl.when(root)
            def _():
                t_copy(r, side, t_back, (z + 7) % 8).wait_send()

    @pl.when(tail)
    def _():
        for r in range(8):
            y_copy(r).wait_send()

    @pl.when(rim_end)
    def _():
        for p in range(4):
            rim_copy(p).wait_send()


def on_device(prior, mapping, triples, factors, transforms):
    mapping = jnp.transpose(mapping, (1, 2, 0))
    vmem = pl.BlockSpec(memory_space=pltpu.VMEM)
    dma = pltpu.SemaphoreType.DMA
    out = pl.pallas_call(
        kernel,
        out_shape=jax.ShapeDtypeStruct((ROWS, PATCH), BF16),
        in_specs=[vmem] * 5,
        out_specs=vmem,
        scratch_shapes=[
            pltpu.VMEM((GROUPS, 4, POINTS), jnp.int32),
            pltpu.VMEM((4, HEAD, POINTS), BF16),
            pltpu.VMEM((8, HEAD, POINTS), BF16),
            pltpu.VMEM((2, 8, 2, HEAD, POINTS), BF16),
            pltpu.VMEM((8, PAIRS, POINTS), BF16),
            pltpu.VMEM((2, 8, 2, PAIRS, POINTS), BF16),
            pltpu.VMEM((PAIRS, POINTS), BF16),
            pltpu.VMEM((2, PAIRS, POINTS), BF16),
            pltpu.VMEM((8, ROWS, BLOCK), BF16),
            pltpu.VMEM((8, ROWS, BLOCK), BF16),
            pltpu.VMEM((FIELDS, BLOCK), F32),
            pltpu.VMEM((MEMBERS * FIELDS, BLOCK), F32),
            pltpu.VMEM((MEMBERS, GROUPS, 8, BLOCK), F32),
            pltpu.VMEM((8, ROWS, BLOCK), BF16),
            pltpu.VMEM((8, ROWS, BLOCK), BF16),
            pltpu.VMEM((ROWS, PATCH), F32),
            pltpu.VMEM((PATCH, BLOCK), BF16),
            pltpu.VMEM((64, BLOCK), F32),
            pltpu.VMEM((4, HEAD, POINTS), F32),
            pltpu.VMEM((BLOCK, BLOCK), BF16),
            pltpu.VMEM((2, POINTS, POINTS), BF16),
            dma((8,)), dma((8,)), dma((16,)), dma((16,)), dma((2,)), dma((4,)), dma((2,)),
            dma((8,)), dma((16,)), dma((16,)), dma((16,)), dma((16,)), dma((16,)),
            dma((8,)), dma((8,)), dma((8,)), dma((8,)),
        ],
        compiler_params=pltpu.CompilerParams(
            collective_id=0, has_side_effects=True, vmem_limit_bytes=62 * 1024 * 1024
        ),
    )(
        prior.reshape(ROWS, PATCH), mapping, jnp.transpose(triples, (1, 0, 2)),
        jnp.transpose(factors, (1, 0, 2)), transforms,
    )
    return out.reshape(LOCAL, FIELDS, PATCH)


def solution(mesh):
    return jax.shard_map(
        on_device,
        mesh=mesh,
        in_specs=(
            P("member", None, "grid"),
            P(None, None, "grid"),
            P("grid", None, "member"),
            P("grid", None, "member"),
            P(None, "grid"),
        ),
        out_specs=P("member", None, "grid"),
        check_vma=False,
    )
```

time: 113 us -> 103 us (0.912)
  the two profiles are of different devices: /device:TPU:65 before, /device:TPU:33 now
where the time goes in v1:
time: 103 us
  Pallas kernels  99.5 us (97%)
  local copies, waits for them, and re-layouts  3.02 us (3%)
    pallas_call x1, Pallas kernels, on_device(): pl.pallas_call(kernel, out_shape=jax.ShapeDtypeStruct((ROWS, PATCH), BF16...  99.5 us
    unnamed x1, local copies, waits for them, and re-layouts  3.02 us

profile of v1, /device:TPU:33, one launch (start us, length us, event | category | flops | bytes accessed | tf_op | source)
XLA Modules:
  0.0 102.5 jit_solution(6555937904068397368)
XLA Ops:
  0.0 99.5 %shard_map.55 = bf16[240,4096]{1,0:T(8,128)(2,1)} custom-call(bf16[240,4096]{1,0:T(8,128)(2,1)} %bitcast.6, s32[8,16,32]{2,1,0:T(8,128)} %bitcast.7, s32[3,1,512]{2,1,0:T(1,128)} %bitcast.8, f32[3,1,512]{2,1,0:T(1,128)} %bitcast.9, f32[1600,128]{1,0:T(8,128)} %trans_ref.1), custom_call_target="tpu_custom_call" | custom-call | tf_op jit(solution)/shard_map/pallas_call | solution.py:483
  99.5 3.0 %copy.7 = bf16[5,48,4096]{2,1,0:T(8,128)(2,1)} copy(bf16[5,48,4096]{2,1,0:T(8,128)(2,1)} %bitcast.5) | data formatting | bytes 3932160

commit v2 on v1

--- a/solution.py
+++ b/solution.py
@@ -20,6 +20,7 @@
 POINTS = 128
 RIM = 16
 PAIRS = 200
+LAG = 3
 HEAD = 16
 
 
@@ -43,14 +44,26 @@
     m, g = lax.axis_index("member"), lax.axis_index("grid")
     z, q = g // 4, g % 4
     yh, c = q // 2, q % 2
-    rim_end = jnp.logical_or(q == 0, q == 3)
-    low_end = q == 3
-    rim_member = jnp.where(low_end, (z + 1) % 8, (z + 7) % 8)
-    far = (z - m + 8) % 8
-    root, tail = far == 0, far == 4
-    passes_on = jnp.logical_and(far != 4, far != 5)
-    ahead = jnp.where(far <= 3, (z + 1) % 8, (z + 7) % 8)
-    near = jnp.logical_or(far == 1, far == 7)
+    half, plane = m // 4, m % 4
+    native = yh == half
+    far = [(z - plane + 8) % 8, (z - plane + 4) % 8]
+    root = z % 4 == plane
+    starts = [jnp.logical_and(far[b] == 0, native) for b in range(2)]
+    passes_on = [jnp.logical_and(far[b] != 4, far[b] != 5) for b in range(2)]
+    ahead = [jnp.where(far[b] <= 3, (z + 1) % 8, (z + 7) % 8) for b in range(2)]
+    hops = [jnp.where(far[b] <= 4, far[b], 8 - far[b]) for b in range(2)]
+    lag = [LAG * (hops[b] + jnp.where(native, 0, 1)) + 1 for b in range(2)]
+    last = jnp.maximum(jnp.maximum(lag[0], lag[1]), 6) + 2
+    pair = jnp.where(c == 1, z * 2 + yh + 1, z * 2 + yh + 15) % 16
+    rim_member = (pair % 2) * 4 + (pair // 2) % 4
+    rim_slot = (pair // 8) * 2 + 1 - c
+    rim_plane = (m + 2) % 8
+    rim_source = (z + 6) % 8
+
+    def rim_from(p):
+        mine = (plane + 4 * (p // 2)) * 2 + half
+        other = (mine + 15) % 16 if p % 2 == 0 else (mine + 1) % 16
+        return other * 2 + (1 - p % 2)
 
     barrier = pltpu.get_barrier_semaphore()
 
@@ -64,19 +77,17 @@
             if s or other:
                 greet((m + s) % 8, z * 4 + ((yh + other) % 2) * 2 + c)
     greet(m, z * 4 + yh * 2 + (1 - c))
-    greet(z, ((m + 7) % 8) * 4 + 3)
-    greet(z, ((m + 1) % 8) * 4)
-
-    @pl.when(rim_end)
-    def _():
-        for p in range(4):
-            greet(rim_member, m * 4 + p)
+    for p in range(4):
+        greet(rim_member, rim_plane * 4 + p)
+        greet(rim_source, rim_from(p))
 
     mapping = map_ref[...].reshape(GROUPS * 16, 32)
     mapping = jnp.concatenate([mapping, jnp.zeros((GROUPS * 16, 96), jnp.int32)], axis=1)
     mapping = jnp.transpose(mapping)
     for to in range(GROUPS):
-        ids_ref[to] = mapping[to * 4 : (to + 1) * 4, :]
+        first = 4 * (to % 4) + 2 * (to // 4)
+        ids_ref[to, 0:2, :] = mapping[first : first + 2, :]
+        ids_ref[to, 2:4, :] = mapping[first + 16 : first + 18, :]
 
     def ids_of(to):
         return jnp.concatenate([ids_ref[to, p : p + 1, :] for p in range(4)], axis=1)
@@ -93,20 +104,22 @@
         zsend[j] = head[:, j * 128 : (j + 1) * 128]
     lane = lax.broadcasted_iota(jnp.int32, (PAIRS, POINTS), 1)
     packed = jnp.zeros((PAIRS, POINTS), F32)
-    base = jnp.where(low_end, POINTS - RIM, 0)
+    base = jnp.where(c == 1, POINTS - RIM, 0)
     for b in range(8):
         block = trans_ref[b * PAIRS : (b + 1) * PAIRS, :]
         tsend[b] = block.astype(BF16)
 
-        @pl.when(root)
-        def _():
-            tbuf[c, b, yh] = trans_ref[b * PAIRS : (b + 1) * PAIRS, :].astype(BF16)
+        for own in range(2):
+
+            @pl.when(starts[own])
+            def _():
+                tbuf[c, b, own] = trans_ref[b * PAIRS : (b + 1) * PAIRS, :].astype(BF16)
 
         block = pltpu.roll(block, (b * RIM - base + POINTS) % POINTS, axis=1)
         packed = jnp.where(lane // RIM == b, block, packed)
     rimsend[...] = packed.astype(BF16)
 
-    pl.semaphore_wait(barrier, jnp.where(rim_end, 29, 25))
+    pl.semaphore_wait(barrier, 31)
 
     def copy(src, dst, send, recv, member, grid):
         return pltpu.make_async_remote_copy(
@@ -116,17 +129,20 @@
 
     def z_copy(s):
         to = (z + s) % 8
-        return copy(zsend.at[to // 2], zrecv.at[z], zs_send.at[s], zs_recv.at[z], m, to * 4 + q)
+        return copy(
+            zsend.at[to // 2], zrecv.at[z % 4, z // 4], zs_send.at[s], zs_recv.at[z], m, to * 4 + q
+        )
 
     def rim_copy(p):
-        which = jnp.where(low_end, 0, 1)
         return copy(
-            rimsend, rimbuf.at[which], rim_send.at[p], rim_recv.at[which], rim_member, m * 4 + p
+            rimsend, rimbuf.at[rim_slot], rim_send.at[p], rim_recv.at[rim_slot],
+            rim_member, rim_plane * 4 + p,
         )
 
     def y_copy(r):
+        own = z // 4
         return copy(
-            tsend.at[r], tbuf.at[c, r, yh], y_send.at[r], t_recv.at[yh * 8 + r],
+            tsend.at[r], tbuf.at[c, r, own], y_send.at[r], t_recv.at[own * 8 + r],
             (m + 4) % 8, z * 4 + (1 - yh) * 2 + c,
         )
 
@@ -147,38 +163,43 @@
     for s in range(1, 8):
         z_copy(s).start()
 
-    @pl.when(tail)
+    @pl.when(jnp.logical_and(root, jnp.logical_not(native)))
     def _():
         for r in range(8):
             y_copy(r).start()
 
-    @pl.when(rim_end)
-    def _():
-        for p in range(4):
-            rim_copy(p).start()
-
-    zrecv[z] = zsend[z // 2]
-
-    def relay(r):
-        for other in range(2):
-            side = (yh + other) % 2
-            if other:
-                t_copy(r, side, t_send, ahead).wait_recv()
-            else:
-
-                @pl.when(jnp.logical_not(root))
+    for b in range(2):
+
+        @pl.when(starts[b])
+        def _():
+            for r in range(8):
+                t_copy(r, b, t_send, (z + 1) % 8).start()
+                t_copy(r, b, t_back, (z + 7) % 8).start()
+                c_copy(c, r, b).start()
+
+    for p in range(4):
+        rim_copy(p).start()
+
+    zrecv[z % 4, z // 4] = zsend[z // 2]
+
+    def tick(t):
+        for b in range(2):
+            r = t - lag[b]
+            due = jnp.logical_and(r >= 0, r < 8)
+
+            @pl.when(jnp.logical_and(due, jnp.logical_not(starts[b])))
+            def _():
+                t_copy(r, b, t_send, ahead[b]).wait_recv()
+
+                @pl.when(passes_on[b])
                 def _():
-                    t_copy(r, side, t_send, ahead).wait_recv()
-
-            @pl.when(passes_on)
-            def _():
-                t_copy(r, side, t_send, ahead).start()
-
-            @pl.when(root)
-            def _():
-                t_copy(r, side, t_back, (z + 7) % 8).start()
-
-            c_copy(c, r, side).start()
+                    t_copy(r, b, t_send, ahead[b]).start()
+
+                @pl.when(far[b] == 0)
+                def _():
+                    t_copy(r, b, t_back, (z + 7) % 8).start()
+
+                c_copy(c, r, b).start()
 
     def turn(s, sign):
         dx = jnp.where(
@@ -205,12 +226,21 @@
                 copy(src.at[to, rows], dst.at[m, rows], send.at[to], recv.at[m], to, g).start()
 
     def param_copy(s, other):
-        to = (m + s) % 8
-        side = (yh + other) % 2
+        to_plane, side = (plane + s) % 4, (yh + other) % 2
         return copy(
-            zrecv.at[to], pbuf.at[c, m, yh], p_send.at[s * 2 + other], p_recv.at[m * 2 + yh],
-            to, z * 4 + side * 2 + c,
-        )
+            zrecv.at[to_plane], pbuf.at[c, m], p_send.at[s * 2 + other], p_recv.at[m],
+            yh * 4 + to_plane, z * 4 + side * 2 + c,
+        )
+
+    def param_sends(act):
+        for t in range(4):
+            for other in range(2):
+                if t or other:
+                    act(param_copy(t, other))
+
+        @pl.when(jnp.logical_not(native))
+        def _():
+            act(param_copy(0, 0))
 
     def pick(s, carry):
         to = turn(s, 1)
@@ -237,35 +267,32 @@
         def _():
             for t in range(1, 8):
                 frm = (z + t) % 8
-                copy(zsend.at[0], zrecv.at[frm], zs_send.at[t], zs_recv.at[frm], m, g).wait_recv()
-            for t in range(8):
-                for other in range(2):
-                    if t or other:
-                        param_copy(t, other).start()
-            pbuf[c, m, yh] = zrecv[m]
-
-        ready = jnp.logical_or(
-            jnp.logical_and(root, s >= 2),
-            jnp.logical_and(near, jnp.logical_or(s == 5, s == 7)),
-        )
-
-        @pl.when(ready)
-        def _():
-            relay(jnp.where(root, s - 2, (s - 5) // 2))
-
+                copy(
+                    zsend.at[0], zrecv.at[frm % 4, frm // 4], zs_send.at[t], zs_recv.at[frm], m, g
+                ).wait_recv()
+            param_sends(lambda sent: sent.start())
+
+            @pl.when(native)
+            def _():
+                pbuf[c, m] = zrecv[plane]
+
+        tick(s)
         return carry
 
     lax.fori_loop(0, 8, pick, 0)
-    relayed = jnp.where(root, 6, jnp.where(near, 2, 0))
-
-    for s in range(8):
-        for other in range(2):
-            if s or other:
-                frm, side = (m + s) % 8, (yh + other) % 2
-                copy(
-                    zrecv.at[frm], pbuf.at[c, frm, side], p_send.at[s * 2 + other],
-                    p_recv.at[frm * 2 + side], frm, z * 4 + side * 2 + c,
-                ).wait_recv()
+
+    def param_wait(frm):
+        copy(
+            zrecv.at[0], pbuf.at[c, frm], p_send.at[0], p_recv.at[frm], frm, z * 4 + half * 2 + c
+        ).wait_recv()
+
+    for s in range(1, 8):
+        param_wait((m + s) % 8)
+
+    @pl.when(jnp.logical_not(native))
+    def _():
+        param_wait(m)
+
     core_copy = copy(
         pbuf.at[c], pbuf.at[c], d_sems.at[0], d_sems.at[1], m, z * 4 + yh * 2 + (1 - c)
     )
@@ -291,12 +318,10 @@
         copy(
             pbuf.at[1 - c], pbuf.at[1 - c], d_sems.at[0], d_sems.at[1], m, z * 4 + yh * 2 + (1 - c)
         ).wait_recv()
-        copy(
-            rimsend, rimbuf.at[0], rim_send.at[0], rim_recv.at[0], z, ((m + 7) % 8) * 4 + 3
-        ).wait_recv()
-        copy(
-            rimsend, rimbuf.at[1], rim_send.at[1], rim_recv.at[1], z, ((m + 1) % 8) * 4
-        ).wait_recv()
+        for p in range(4):
+            copy(
+                rimsend, rimbuf.at[p], rim_send.at[p], rim_recv.at[p], rim_source, rim_from(p)
+            ).wait_recv()
         offset = (z % 2) * 64 + q * 16
         lane16 = lax.broadcasted_iota(jnp.int32, (HEAD, POINTS), 1) // 16
         depth = lax.broadcasted_iota(jnp.int32, (BLOCK, POINTS), 0)
@@ -310,7 +335,8 @@
             column = jnp.zeros((BLOCK, POINTS), F32)
             for w in range(3):
                 point = in_order[w : w + 1, :].astype(jnp.int32) + (p * POINTS - RIM)
-                column = column + jnp.where(depth == point, in_order[w + 3 : w + 4, :], 0.0)
+                hit = jnp.logical_and(depth == point, depth // 256 == p // 2)
+                column = column + jnp.where(hit, in_order[w + 3 : w + 4, :], 0.0)
             spread[:, p * POINTS : (p + 1) * POINTS] = column.astype(BF16)
 
     rim_depth = lax.broadcasted_iota(jnp.int32, (POINTS, POINTS), 0)
@@ -320,46 +346,45 @@
             c_copy(1 - c, r, side).wait_recv()
         shifted = rim_depth - r * RIM
         inside = rim_depth // RIM == r
-        for end, p, back in ((0, 0, 0), (1, 3, POINTS + RIM)):
+        for p in range(4):
             column = jnp.zeros((POINTS, POINTS), F32)
             for w in range(3):
-                point = params[p, w : w + 1, :].astype(jnp.int32) - back
+                point = params[p, w : w + 1, :].astype(jnp.int32) - (p % 2) * (POINTS + RIM)
                 hit = jnp.logical_and(inside, shifted == point)
                 column = column + jnp.where(hit, params[p, w + 3 : w + 4, :], 0.0)
-            spread_rim[end] = column.astype(BF16)
+            spread_rim[p] = column.astype(BF16)
         rows = jnp.concatenate([tbuf[p % 2, r, p // 2] for p in range(4)], axis=1)
-        main = jnp.dot(rows, spread[...], preferred_element_type=F32)
-        lo = jnp.dot(rimbuf[0], spread_rim[0], preferred_element_type=F32)
-        hi = jnp.dot(rimbuf[1], spread_rim[1], preferred_element_type=F32)
-        whole = jnp.concatenate(
-            [main[:, 0:128] + lo, main[:, 128:384], main[:, 384:512] + hi], axis=1
-        )
+        whole = jnp.dot(rows, spread[...], preferred_element_type=F32)
+        ends = [
+            jnp.dot(rimbuf[p], spread_rim[p], preferred_element_type=F32) for p in range(4)
+        ]
+        whole = whole + jnp.concatenate(ends, axis=1)
         whole = whole.astype(BF16).astype(F32)
         for k in range(LOCAL):
             for to in range(GROUPS):
                 row = k * MEMBERS + to * LOCAL
                 weights[r * LOCAL + k, to, 0:LOCAL, :] = whole[row : row + LOCAL, :]
 
-    def arrive(r, carry):
-        @pl.when(jnp.logical_and(r >= relayed, r < 8))
-        def _():
-            relay(r)
-
-        @pl.when(r == 1)
+    def arrive(t, carry):
+        tick(t)
+
+        @pl.when(t == 8)
         def _():
             prepare()
 
-        @pl.when(r < 4)
-        def _():
-            add_up((r + 7) % 8)
-
-        @pl.when(r >= 1)
-        def _():
-            blend(r - 1)
+        @pl.when(t < 12)
+        def _():
+            add_up((t + 7) % 8)
+
+        r = t - last
+
+        @pl.when(jnp.logical_and(r >= 0, r < 8))
+        def _():
+            blend(r)
 
         return carry
 
-    lax.fori_loop(0, 9, arrive, 0)
+    lax.fori_loop(8, 8 + 5 * LAG + 3, arrive, 0)
 
     def add_rest(s, carry):
         add_up(s)
@@ -448,32 +473,27 @@
         z_copy(s).wait_send()
         state_copy((m + s) % 8).wait_send()
         return_copy((m + s) % 8).wait_send()
-    for s in range(8):
-        for other in range(2):
-            if s or other:
-                param_copy(s, other).wait_send()
+    param_sends(lambda sent: sent.wait_send())
     core_copy.wait_send()
     for r in range(8):
-        for side in range(2):
-            c_copy(c, r, side).wait_send()
-
-            @pl.when(passes_on)
+        for b in range(2):
+            c_copy(c, r, b).wait_send()
+
+            @pl.when(passes_on[b])
             def _():
-                t_copy(r, side, t_send, ahead).wait_send()
-
-            @pl.when(root)
+                t_copy(r, b, t_send, ahead[b]).wait_send()
+
+            @pl.when(far[b] == 0)
             def _():
-                t_copy(r, side, t_back, (z + 7) % 8).wait_send()
-
-    @pl.when(tail)
+                t_copy(r, b, t_back, (z + 7) % 8).wait_send()
+
+    @pl.when(jnp.logical_and(root, jnp.logical_not(native)))
     def _():
         for r in range(8):
             y_copy(r).wait_send()
 
-    @pl.when(rim_end)
-    def _():
-        for p in range(4):
-            rim_copy(p).wait_send()
+    for p in range(4):
+        rim_copy(p).wait_send()
 
 
 def on_device(prior, mapping, triples, factors, transforms):
@@ -488,12 +508,12 @@
         scratch_shapes=[
             pltpu.VMEM((GROUPS, 4, POINTS), jnp.int32),
             pltpu.VMEM((4, HEAD, POINTS), BF16),
-            pltpu.VMEM((8, HEAD, POINTS), BF16),
+            pltpu.VMEM((4, 2, HEAD, POINTS), BF16),
             pltpu.VMEM((2, 8, 2, HEAD, POINTS), BF16),
             pltpu.VMEM((8, PAIRS, POINTS), BF16),
             pltpu.VMEM((2, 8, 2, PAIRS, POINTS), BF16),
             pltpu.VMEM((PAIRS, POINTS), BF16),
-            pltpu.VMEM((2, PAIRS, POINTS), BF16),
+            pltpu.VMEM((4, PAIRS, POINTS), BF16),
             pltpu.VMEM((8, ROWS, BLOCK), BF16),
             pltpu.VMEM((8, ROWS, BLOCK), BF16),
             pltpu.VMEM((FIELDS, BLOCK), F32),
@@ -506,8 +526,8 @@
             pltpu.VMEM((64, BLOCK), F32),
             pltpu.VMEM((4, HEAD, POINTS), F32),
             pltpu.VMEM((BLOCK, BLOCK), BF16),
-            pltpu.VMEM((2, POINTS, POINTS), BF16),
-            dma((8,)), dma((8,)), dma((16,)), dma((16,)), dma((2,)), dma((4,)), dma((2,)),
+            pltpu.VMEM((4, POINTS, POINTS), BF16),
+            dma((8,)), dma((8,)), dma((8,)), dma((8,)), dma((2,)), dma((4,)), dma((4,)),
             dma((8,)), dma((16,)), dma((16,)), dma((16,)), dma((16,)), dma((16,)),
             dma((8,)), dma((8,)), dma((8,)), dma((8,)),
         ],

time: 103 us -> 103 us (level)
  the two profiles are of different devices: /device:TPU:33 before, /device:TPU:1 now
where the time goes in v2:
time: 103 us
  Pallas kernels  99.6 us (97%)
  local copies, waits for them, and re-layouts  3.02 us (3%)
    pallas_call x1, Pallas kernels, on_device(): pl.pallas_call(kernel, out_shape=jax.ShapeDtypeStruct((ROWS, PATCH), BF16...  99.6 us
    unnamed x1, local copies, waits for them, and re-layouts  3.02 us

profile of v2, /device:TPU:1, one launch (start us, length us, event | category | flops | bytes accessed | tf_op | source)
XLA Modules:
  0.0 102.6 jit_solution(7866027883248729766)
XLA Ops:
  0.0 99.6 %shard_map.55 = bf16[240,4096]{1,0:T(8,128)(2,1)} custom-call(bf16[240,4096]{1,0:T(8,128)(2,1)} %bitcast.6, s32[8,16,32]{2,1,0:T(8,128)} %bitcast.7, s32[3,1,512]{2,1,0:T(1,128)} %bitcast.8, f32[3,1,512]{2,1,0:T(1,128)} %bitcast.9, f32[1600,128]{1,0:T(8,128)} %trans_ref.1), custom_call_target="tpu_custom_call" | custom-call | tf_op jit(solution)/shard_map/pallas_call | solution.py:503
  99.6 3.0 %copy.7 = bf16[5,48,4096]{2,1,0:T(8,128)(2,1)} copy(bf16[5,48,4096]{2,1,0:T(8,128)(2,1)} %bitcast.5) | data formatting | bytes 3932160

commit v3 on v2

--- a/solution.py
+++ b/solution.py
@@ -36,9 +36,9 @@
 
 def kernel(
     prior_ref, map_ref, pts_ref, fac_ref, trans_ref, out_ref,
-    ids_ref, zsend, zrecv, pbuf, tsend, tbuf, rimsend, rimbuf, picked, gathered, mean, dev,
+    ids_ref, zsend, zrecv, pbuf, tsend, tbuf, rimsend, picked, gathered, mean, dev,
     weights, result, returned, total, oh, hi_ref, params, spread, spread_rim,
-    zs_send, zs_recv, p_send, p_recv, d_sems, rim_send, rim_recv, y_send, t_send, t_back,
+    zs_send, zs_recv, p_send, p_recv, d_sems, rim_send, y_send, t_send, t_back,
     t_recv, c_send, c_recv, st_send, st_recv, rt_send, rt_recv,
 ):
     m, g = lax.axis_index("member"), lax.axis_index("grid")
@@ -53,17 +53,17 @@
     ahead = [jnp.where(far[b] <= 3, (z + 1) % 8, (z + 7) % 8) for b in range(2)]
     hops = [jnp.where(far[b] <= 4, far[b], 8 - far[b]) for b in range(2)]
     lag = [LAG * (hops[b] + jnp.where(native, 0, 1)) + 1 for b in range(2)]
-    last = jnp.maximum(jnp.maximum(lag[0], lag[1]), 6) + 2
+    last = jnp.maximum(lag[0], lag[1]) + 6
     pair = jnp.where(c == 1, z * 2 + yh + 1, z * 2 + yh + 15) % 16
     rim_member = (pair % 2) * 4 + (pair // 2) % 4
-    rim_slot = (pair // 8) * 2 + 1 - c
-    rim_plane = (m + 2) % 8
-    rim_source = (z + 6) % 8
-
-    def rim_from(p):
-        mine = (plane + 4 * (p // 2)) * 2 + half
-        other = (mine + 15) % 16 if p % 2 == 0 else (mine + 1) % 16
-        return other * 2 + (1 - p % 2)
+    level = pair // 2 == z
+    rim_across = rim_member == (m + 4) % 8
+    rim_here = jnp.logical_and(rim_member == m, level)
+    rim_along = jnp.logical_and(rim_member == m, jnp.logical_not(level))
+    mine = z * 2 + half
+    rim_pair = jnp.where(c == 0, mine + 1, mine + 15) % 16
+    rim_in = jnp.logical_and(jnp.logical_and(root, native), rim_pair // 2 != z)
+    rim_out = jnp.logical_and(rim_across, jnp.logical_not(level))
 
     barrier = pltpu.get_barrier_semaphore()
 
@@ -77,9 +77,14 @@
             if s or other:
                 greet((m + s) % 8, z * 4 + ((yh + other) % 2) * 2 + c)
     greet(m, z * 4 + yh * 2 + (1 - c))
-    for p in range(4):
-        greet(rim_member, rim_plane * 4 + p)
-        greet(rim_source, rim_from(p))
+
+    @pl.when(rim_out)
+    def _():
+        greet((m + 4) % 8, pair * 2 + c)
+
+    @pl.when(rim_in)
+    def _():
+        greet((m + 4) % 8, rim_pair * 2 + c)
 
     mapping = map_ref[...].reshape(GROUPS * 16, 32)
     mapping = jnp.concatenate([mapping, jnp.zeros((GROUPS * 16, 96), jnp.int32)], axis=1)
@@ -119,7 +124,7 @@
         packed = jnp.where(lane // RIM == b, block, packed)
     rimsend[...] = packed.astype(BF16)
 
-    pl.semaphore_wait(barrier, 31)
+    pl.semaphore_wait(barrier, 23 + jnp.where(rim_out, 1, 0) + jnp.where(rim_in, 1, 0))
 
     def copy(src, dst, send, recv, member, grid):
         return pltpu.make_async_remote_copy(
@@ -133,28 +138,31 @@
             zsend.at[to // 2], zrecv.at[z % 4, z // 4], zs_send.at[s], zs_recv.at[z], m, to * 4 + q
         )
 
-    def rim_copy(p):
+    def rim_copy(member, grid):
+        dst = pair // 8
         return copy(
-            rimsend, rimbuf.at[rim_slot], rim_send.at[p], rim_recv.at[rim_slot],
-            rim_member, rim_plane * 4 + p,
-        )
+            rimsend, tbuf.at[c, 8, dst], rim_send.at[0], t_recv.at[dst * 9 + 8], member, grid
+        )
+
+    across = rim_copy((m + 4) % 8, pair * 2 + c)
+    along = rim_copy(m, (pair // 2) * 4 + yh * 2 + c)
 
     def y_copy(r):
         own = z // 4
         return copy(
-            tsend.at[r], tbuf.at[c, r, own], y_send.at[r], t_recv.at[own * 8 + r],
+            tsend.at[r], tbuf.at[c, r, own], y_send.at[r], t_recv.at[own * 9 + r],
             (m + 4) % 8, z * 4 + (1 - yh) * 2 + c,
         )
 
     def t_copy(r, side, sems, to):
-        slot = side * 8 + r
+        slot = side * 9 + r
         return copy(
             tbuf.at[c, r, side], tbuf.at[c, r, side], sems.at[slot], t_recv.at[slot],
             m, to * 4 + q,
         )
 
     def c_copy(core, r, side):
-        slot = side * 8 + r
+        slot = side * 9 + r
         return copy(
             tbuf.at[core, r, side], tbuf.at[core, r, side], c_send.at[slot], c_recv.at[slot],
             m, z * 4 + yh * 2 + (1 - c),
@@ -168,28 +176,45 @@
         for r in range(8):
             y_copy(r).start()
 
+    @pl.when(rim_across)
+    def _():
+        across.start()
+
+    @pl.when(rim_along)
+    def _():
+        along.start()
+
+    @pl.when(rim_here)
+    def _():
+        tbuf[c, 8, pair // 8] = rimsend[...]
+
+    def spread_out(r, b):
+        t_copy(r, b, t_send, (z + 1) % 8).start()
+        t_copy(r, b, t_back, (z + 7) % 8).start()
+        c_copy(c, r, b).start()
+
     for b in range(2):
 
         @pl.when(starts[b])
         def _():
-            for r in range(8):
-                t_copy(r, b, t_send, (z + 1) % 8).start()
-                t_copy(r, b, t_back, (z + 7) % 8).start()
-                c_copy(c, r, b).start()
-
-    for p in range(4):
-        rim_copy(p).start()
+            for r in range(4):
+                spread_out(r, b)
 
     zrecv[z % 4, z // 4] = zsend[z // 2]
 
     def tick(t):
         for b in range(2):
-            r = t - lag[b]
-            due = jnp.logical_and(r >= 0, r < 8)
+            place_in = t - lag[b]
+            due = jnp.logical_and(place_in >= 0, place_in < 9)
+            r = jnp.where(place_in < 4, place_in, jnp.where(place_in == 4, 8, place_in - 1))
 
             @pl.when(jnp.logical_and(due, jnp.logical_not(starts[b])))
             def _():
-                t_copy(r, b, t_send, ahead[b]).wait_recv()
+                here = jnp.logical_and(jnp.logical_and(r == 8, rim_here), far[b] == 0)
+
+                @pl.when(jnp.logical_not(here))
+                def _():
+                    t_copy(r, b, t_send, ahead[b]).wait_recv()
 
                 @pl.when(passes_on[b])
                 def _():
@@ -200,6 +225,13 @@
                     t_copy(r, b, t_back, (z + 7) % 8).start()
 
                 c_copy(c, r, b).start()
+
+            @pl.when(jnp.logical_and(t == 1, starts[b]))
+            def _():
+                t_copy(8, b, t_send, ahead[b]).wait_recv()
+                spread_out(8, b)
+                for r in range(4, 8):
+                    spread_out(r, b)
 
     def turn(s, sign):
         dx = jnp.where(
@@ -318,10 +350,6 @@
         copy(
             pbuf.at[1 - c], pbuf.at[1 - c], d_sems.at[0], d_sems.at[1], m, z * 4 + yh * 2 + (1 - c)
         ).wait_recv()
-        for p in range(4):
-            copy(
-                rimsend, rimbuf.at[p], rim_send.at[p], rim_recv.at[p], rim_source, rim_from(p)
-            ).wait_recv()
         offset = (z % 2) * 64 + q * 16
         lane16 = lax.broadcasted_iota(jnp.int32, (HEAD, POINTS), 1) // 16
         depth = lax.broadcasted_iota(jnp.int32, (BLOCK, POINTS), 0)
@@ -341,7 +369,7 @@
 
     rim_depth = lax.broadcasted_iota(jnp.int32, (POINTS, POINTS), 0)
 
-    def blend(r):
+    def blend(r, carry):
         for side in range(2):
             c_copy(1 - c, r, side).wait_recv()
         shifted = rim_depth - r * RIM
@@ -356,7 +384,8 @@
         rows = jnp.concatenate([tbuf[p % 2, r, p // 2] for p in range(4)], axis=1)
         whole = jnp.dot(rows, spread[...], preferred_element_type=F32)
         ends = [
-            jnp.dot(rimbuf[p], spread_rim[p], preferred_element_type=F32) for p in range(4)
+            jnp.dot(tbuf[1 - p % 2, 8, p // 2], spread_rim[p], preferred_element_type=F32)
+            for p in range(4)
         ]
         whole = whole + jnp.concatenate(ends, axis=1)
         whole = whole.astype(BF16).astype(F32)
@@ -364,6 +393,7 @@
             for to in range(GROUPS):
                 row = k * MEMBERS + to * LOCAL
                 weights[r * LOCAL + k, to, 0:LOCAL, :] = whole[row : row + LOCAL, :]
+        return carry
 
     def arrive(t, carry):
         tick(t)
@@ -376,15 +406,20 @@
         def _():
             add_up((t + 7) % 8)
 
-        r = t - last
-
-        @pl.when(jnp.logical_and(r >= 0, r < 8))
-        def _():
-            blend(r)
-
-        return carry
-
-    lax.fori_loop(8, 8 + 5 * LAG + 3, arrive, 0)
+        j = t - last
+
+        @pl.when(j == 0)
+        def _():
+            for side in range(2):
+                c_copy(1 - c, 8, side).wait_recv()
+
+        @pl.when(jnp.logical_and(j >= 0, j < 4))
+        def _():
+            lax.fori_loop(2 * j, 2 * j + 2, blend, 0)
+
+        return carry
+
+    lax.fori_loop(8, 5 * LAG + 11, arrive, 0)
 
     def add_rest(s, carry):
         add_up(s)
@@ -475,7 +510,7 @@
         return_copy((m + s) % 8).wait_send()
     param_sends(lambda sent: sent.wait_send())
     core_copy.wait_send()
-    for r in range(8):
+    for r in range(9):
         for b in range(2):
             c_copy(c, r, b).wait_send()
 
@@ -492,8 +527,13 @@
         for r in range(8):
             y_copy(r).wait_send()
 
-    for p in range(4):
-        rim_copy(p).wait_send()
+    @pl.when(rim_across)
+    def _():
+        across.wait_send()
+
+    @pl.when(rim_along)
+    def _():
+        along.wait_send()
 
 
 def on_device(prior, mapping, triples, factors, transforms):
@@ -511,9 +551,8 @@
             pltpu.VMEM((4, 2, HEAD, POINTS), BF16),
             pltpu.VMEM((2, 8, 2, HEAD, POINTS), BF16),
             pltpu.VMEM((8, PAIRS, POINTS), BF16),
-            pltpu.VMEM((2, 8, 2, PAIRS, POINTS), BF16),
+            pltpu.VMEM((2, 9, 2, PAIRS, POINTS), BF16),
             pltpu.VMEM((PAIRS, POINTS), BF16),
-            pltpu.VMEM((4, PAIRS, POINTS), BF16),
             pltpu.VMEM((8, ROWS, BLOCK), BF16),
             pltpu.VMEM((8, ROWS, BLOCK), BF16),
             pltpu.VMEM((FIELDS, BLOCK), F32),
@@ -527,8 +566,8 @@
             pltpu.VMEM((4, HEAD, POINTS), F32),
             pltpu.VMEM((BLOCK, BLOCK), BF16),
             pltpu.VMEM((4, POINTS, POINTS), BF16),
-            dma((8,)), dma((8,)), dma((8,)), dma((8,)), dma((2,)), dma((4,)), dma((4,)),
-            dma((8,)), dma((16,)), dma((16,)), dma((16,)), dma((16,)), dma((16,)),
+            dma((8,)), dma((8,)), dma((8,)), dma((8,)), dma((2,)), dma((1,)),
+            dma((8,)), dma((18,)), dma((18,)), dma((18,)), dma((18,)), dma((18,)),
             dma((8,)), dma((8,)), dma((8,)), dma((8,)),
         ],
         compiler_params=pltpu.CompilerParams(

time: 103 us -> 85.1 us (0.83)
  the two profiles are of different devices: /device:TPU:1 before, /device:TPU:34 now
where the time goes in v3:
time: 85.1 us; the launch traced here: 85 us
  Pallas kernels  82 us (96%)
  local copies, waits for them, and re-layouts  3.02 us (4%)
    pallas_call x1, Pallas kernels, on_device(): pl.pallas_call(kernel, out_shape=jax.ShapeDtypeStruct((ROWS, PATCH), BF16...  82 us
    unnamed x1, local copies, waits for them, and re-layouts  3.02 us

profile of v3, /device:TPU:34, one launch (start us, length us, event | category | flops | bytes accessed | tf_op | source)
XLA Modules:
  0.0 85.0 jit_solution(12783694290538452803)
XLA Ops:
  0.0 82.0 %shard_map.55 = bf16[240,4096]{1,0:T(8,128)(2,1)} custom-call(bf16[240,4096]{1,0:T(8,128)(2,1)} %bitcast.6, s32[8,16,32]{2,1,0:T(8,128)} %bitcast.7, s32[3,1,512]{2,1,0:T(1,128)} %bitcast.8, f32[3,1,512]{2,1,0:T(1,128)} %bitcast.9, f32[1600,128]{1,0:T(8,128)} %trans_ref.1), custom_call_target="tpu_custom_call" | custom-call | tf_op jit(solution)/shard_map/pallas_call | solution.py:543
  82.0 3.0 %copy.7 = bf16[5,48,4096]{2,1,0:T(8,128)(2,1)} copy(bf16[5,48,4096]{2,1,0:T(8,128)(2,1)} %bitcast.5) | data formatting | bytes 3932160

commit v4 on v3

--- a/solution.py
+++ b/solution.py
@@ -20,23 +20,24 @@
 POINTS = 128
 RIM = 16
 PAIRS = 200
-LAG = 3
+LAG = 2
 HEAD = 16
 
 
 def onehot_into(oh_ref, hi_ref, ids):
+    width = ids.shape[1]
     hi, lo = ids >> 6, ids & 63
-    level = lax.broadcasted_iota(jnp.int32, (64, BLOCK), 0)
-    hi_ref[...] = jnp.where(level == hi, 1.0, 0.0).astype(F32)
-    low = jnp.where(level == lo, 1.0, 0.0).astype(BF16).reshape(4, 16, BLOCK)
+    level = lax.broadcasted_iota(jnp.int32, (64, width), 0)
+    hi_ref[:, 0:width] = jnp.where(level == hi, 1.0, 0.0).astype(F32)
+    low = jnp.where(level == lo, 1.0, 0.0).astype(BF16).reshape(4, 16, width)
     for h in range(64):
-        row = jnp.broadcast_to(hi_ref[h : h + 1, :], (16, BLOCK)).astype(BF16)
-        oh_ref[h * 64 : (h + 1) * 64, :] = (low * row[None]).reshape(64, BLOCK)
+        row = jnp.broadcast_to(hi_ref[h : h + 1, 0:width], (16, width)).astype(BF16)
+        oh_ref[h * 64 : (h + 1) * 64, 0:width] = (low * row[None]).reshape(64, width)
 
 
 def kernel(
     prior_ref, map_ref, pts_ref, fac_ref, trans_ref, out_ref,
-    ids_ref, zsend, zrecv, pbuf, tsend, tbuf, rimsend, picked, gathered, mean, dev,
+    ids_ref, zsend, zrecv, pbuf, tsend, tbuf, rimsend, picked, gathered, mean, mean_of, dev,
     weights, result, returned, total, oh, hi_ref, params, spread, spread_rim,
     zs_send, zs_recv, p_send, p_recv, d_sems, rim_send, y_send, t_send, t_back,
     t_recv, c_send, c_recv, st_send, st_recv, rt_send, rt_recv,
@@ -53,7 +54,9 @@
     ahead = [jnp.where(far[b] <= 3, (z + 1) % 8, (z + 7) % 8) for b in range(2)]
     hops = [jnp.where(far[b] <= 4, far[b], 8 - far[b]) for b in range(2)]
     lag = [LAG * (hops[b] + jnp.where(native, 0, 1)) + 1 for b in range(2)]
-    last = jnp.maximum(lag[0], lag[1]) + 6
+    near = jnp.where(hops[0] <= hops[1], 0, 1)
+    last = jnp.maximum(jnp.minimum(lag[0], lag[1]), 2) + 6
+    turned = jnp.maximum(last + 4, 12)
     pair = jnp.where(c == 1, z * 2 + yh + 1, z * 2 + yh + 15) % 16
     rim_member = (pair % 2) * 4 + (pair // 2) % 4
     level = pair // 2 == z
@@ -91,11 +94,14 @@
     mapping = jnp.transpose(mapping)
     for to in range(GROUPS):
         first = 4 * (to % 4) + 2 * (to // 4)
-        ids_ref[to, 0:2, :] = mapping[first : first + 2, :]
-        ids_ref[to, 2:4, :] = mapping[first + 16 : first + 18, :]
+        ids_ref[to, 0] = mapping[first : first + 2, :]
+        ids_ref[to, 1] = mapping[first + 16 : first + 18, :]
+
+    def half_ids(to, b):
+        return jnp.concatenate([ids_ref[to, b, p : p + 1, :] for p in range(2)], axis=1)
 
     def ids_of(to):
-        return jnp.concatenate([ids_ref[to, p : p + 1, :] for p in range(4)], axis=1)
+        return jnp.concatenate([half_ids(to, b) for b in range(2)], axis=1)
 
     raw = [fac_ref[w] for w in range(3)]
     raw_sum = raw[0] + raw[1] + raw[2]
@@ -247,15 +253,21 @@
     def state_copy(to):
         return copy(picked.at[to], gathered.at[m], st_send.at[to], st_recv.at[m], to, g)
 
-    def return_copy(to):
-        return copy(result.at[to], returned.at[m], rt_send.at[to], rt_recv.at[m], to, g)
-
-    def start_pieces(src, dst, send, recv, turns):
+    def return_copy(to, b):
+        return copy(
+            result.at[b, to], returned.at[b, m], rt_send.at[b * 8 + to], rt_recv.at[b * 8 + m],
+            to, g,
+        )
+
+    def start_pieces(src, dst, send, recv, turns, shift=0):
         for k in range(LOCAL):
             for t in turns:
                 to = turn(t, 1)
                 rows = pl.ds(k * FIELDS, FIELDS)
-                copy(src.at[to, rows], dst.at[m, rows], send.at[to], recv.at[m], to, g).start()
+                copy(
+                    src.at[to, rows], dst.at[m, rows], send.at[shift + to], recv.at[shift + m],
+                    to, g,
+                ).start()
 
     def param_copy(s, other):
         to_plane, side = (plane + s) % 4, (yh + other) % 2
@@ -352,7 +364,7 @@
         ).wait_recv()
         offset = (z % 2) * 64 + q * 16
         lane16 = lax.broadcasted_iota(jnp.int32, (HEAD, POINTS), 1) // 16
-        depth = lax.broadcasted_iota(jnp.int32, (BLOCK, POINTS), 0)
+        depth = lax.broadcasted_iota(jnp.int32, (2 * POINTS, POINTS), 0)
         for p in range(4):
             in_order = jnp.zeros((HEAD, POINTS), F32)
             for r in range(8):
@@ -360,40 +372,38 @@
                 tile = pltpu.roll(tile, (r * 16 - offset + POINTS) % POINTS, axis=1)
                 in_order = jnp.where(lane16 == r, tile, in_order)
             params[p] = in_order
-            column = jnp.zeros((BLOCK, POINTS), F32)
+            column = jnp.zeros((2 * POINTS, POINTS), F32)
             for w in range(3):
-                point = in_order[w : w + 1, :].astype(jnp.int32) + (p * POINTS - RIM)
-                hit = jnp.logical_and(depth == point, depth // 256 == p // 2)
-                column = column + jnp.where(hit, in_order[w + 3 : w + 4, :], 0.0)
-            spread[:, p * POINTS : (p + 1) * POINTS] = column.astype(BF16)
+                point = in_order[w : w + 1, :].astype(jnp.int32) + ((p % 2) * POINTS - RIM)
+                column = column + jnp.where(depth == point, in_order[w + 3 : w + 4, :], 0.0)
+            spread[p // 2, :, (p % 2) * POINTS : (p % 2 + 1) * POINTS] = column.astype(BF16)
 
     rim_depth = lax.broadcasted_iota(jnp.int32, (POINTS, POINTS), 0)
 
-    def blend(r, carry):
-        for side in range(2):
-            c_copy(1 - c, r, side).wait_recv()
+    def blend(r, b):
+        c_copy(1 - c, r, b).wait_recv()
         shifted = rim_depth - r * RIM
         inside = rim_depth // RIM == r
-        for p in range(4):
+        for p in range(2):
             column = jnp.zeros((POINTS, POINTS), F32)
             for w in range(3):
-                point = params[p, w : w + 1, :].astype(jnp.int32) - (p % 2) * (POINTS + RIM)
+                point = params[2 * b + p, w : w + 1, :].astype(jnp.int32) - p * (POINTS + RIM)
                 hit = jnp.logical_and(inside, shifted == point)
-                column = column + jnp.where(hit, params[p, w + 3 : w + 4, :], 0.0)
+                column = column + jnp.where(hit, params[2 * b + p, w + 3 : w + 4, :], 0.0)
             spread_rim[p] = column.astype(BF16)
-        rows = jnp.concatenate([tbuf[p % 2, r, p // 2] for p in range(4)], axis=1)
-        whole = jnp.dot(rows, spread[...], preferred_element_type=F32)
+        rows = jnp.concatenate([tbuf[p, r, b] for p in range(2)], axis=1)
+        whole = jnp.dot(rows, spread[b], preferred_element_type=F32)
         ends = [
-            jnp.dot(tbuf[1 - p % 2, 8, p // 2], spread_rim[p], preferred_element_type=F32)
-            for p in range(4)
+            jnp.dot(tbuf[1 - p, 8, b], spread_rim[p], preferred_element_type=F32)
+            for p in range(2)
         ]
         whole = whole + jnp.concatenate(ends, axis=1)
         whole = whole.astype(BF16).astype(F32)
         for k in range(LOCAL):
             for to in range(GROUPS):
                 row = k * MEMBERS + to * LOCAL
-                weights[r * LOCAL + k, to, 0:LOCAL, :] = whole[row : row + LOCAL, :]
-        return carry
+                weights[b, r * LOCAL + k, to, 0:LOCAL, :] = whole[row : row + LOCAL, :]
+        return b
 
     def arrive(t, carry):
         tick(t)
@@ -410,104 +420,124 @@
 
         @pl.when(j == 0)
         def _():
-            for side in range(2):
-                c_copy(1 - c, 8, side).wait_recv()
+            c_copy(1 - c, 8, near).wait_recv()
 
         @pl.when(jnp.logical_and(j >= 0, j < 4))
         def _():
-            lax.fori_loop(2 * j, 2 * j + 2, blend, 0)
+            lax.fori_loop(2 * j, 2 * j + 2, blend, near)
 
         return carry
 
-    lax.fori_loop(8, 5 * LAG + 11, arrive, 0)
+    lax.fori_loop(8, turned, arrive, 0)
 
     def add_rest(s, carry):
         add_up(s)
         return carry
 
     lax.fori_loop(3, 7, add_rest, 0)
-    mean[...] = mean[...] / MEMBERS
+    for b in range(2):
+        mean_of[b] = mean[:, b * 256 : (b + 1) * 256] / MEMBERS
 
     def deviate(r, carry):
         for k in range(LOCAL):
-            x = gathered[r, k * FIELDS : (k + 1) * FIELDS, :].astype(F32)
             row = pl.multiple_of((r * LOCAL + k) * FIELDS, 8)
-            dev[pl.ds(row, FIELDS), :] = (x - mean[...]).astype(BF16).astype(F32)
+            for b in range(2):
+                x = gathered[r, k * FIELDS : (k + 1) * FIELDS, b * 256 : (b + 1) * 256]
+                difference = x.astype(F32) - mean_of[b]
+                dev[b, pl.ds(row, FIELDS), :] = difference.astype(BF16).astype(F32)
         return carry
 
     lax.fori_loop(0, GROUPS, deviate, 0)
 
-    def analyse(s, carry):
+    def analyse(i, carry):
+        s, b = i % 8, jnp.where(i < 8, near, 1 - near)
         to = turn(s, 1)
-        for b in range(4):
-            lanes = slice(b * 128, (b + 1) * 128)
+
+        @pl.when(i < 8)
+        def _():
+            tick(turned + i)
+
+        @pl.when(i == 8)
+        def _():
+            c_copy(1 - c, 8, b).wait_recv()
+            lax.fori_loop(0, 8, blend, b)
+
+        for half_lanes in range(2):
+            lanes = slice(half_lanes * 128, (half_lanes + 1) * 128)
 
             def step(i, sums):
                 sums = list(sums)
                 for k in range(8):
                     row = pl.multiple_of((i * 8 + k) * FIELDS, 8)
-                    x = dev[pl.ds(row, FIELDS), lanes]
+                    x = dev[b, pl.ds(row, FIELDS), lanes]
                     for j in range(LOCAL):
-                        sums[j] = sums[j] + x * weights[i * 8 + k, to, j : j + 1, lanes]
+                        sums[j] = sums[j] + x * weights[b, i * 8 + k, to, j : j + 1, lanes]
                 return tuple(sums)
 
             sums = lax.fori_loop(
                 0, MEMBERS // 8, step, tuple(jnp.zeros((FIELDS, 128), F32) for _ in range(LOCAL))
             )
             for j in range(LOCAL):
-                value = (sums[j] + mean[:, lanes]).astype(BF16)
+                value = (sums[j] + mean_of[b, :, lanes]).astype(BF16)
 
                 @pl.when(s < 7)
                 def _():
-                    result[to, j * FIELDS : (j + 1) * FIELDS, lanes] = value
+                    result[b, to, j * FIELDS : (j + 1) * FIELDS, lanes] = value
 
                 @pl.when(s == 7)
                 def _():
-                    returned[m, j * FIELDS : (j + 1) * FIELDS, lanes] = value
+                    returned[b, m, j * FIELDS : (j + 1) * FIELDS, lanes] = value
 
         @pl.when(s < 3)
         def _():
-            return_copy(to).start()
+            return_copy(to, b).start()
 
         @pl.when(s == 4)
         def _():
-            start_pieces(result, returned, rt_send, rt_recv, (3, 4))
+            start_pieces(result.at[b], returned.at[b], rt_send, rt_recv, (3, 4), b * 8)
 
         @pl.when(s == 6)
         def _():
-            start_pieces(result, returned, rt_send, rt_recv, (5, 6))
+            start_pieces(result.at[b], returned.at[b], rt_send, rt_recv, (5, 6), b * 8)
 
         return carry
 
-    lax.fori_loop(0, 8, analyse, 0)
+    lax.fori_loop(0, 16, analyse, 0)
 
     total[...] = jnp.zeros((ROWS, PATCH), F32)
 
     def place(i, carry):
         s = (i + 7) % 8
         frm = turn(s, -1)
+        first = (z - frm % 4 + 8) % 8
+        second = (first + 4) % 8
+        close = jnp.minimum(first, 8 - first) <= jnp.minimum(second, 8 - second)
+        b = jnp.where(close, i // 8, 1 - i // 8)
 
         @pl.when(s < 7)
         def _():
             copy(
-                result.at[frm], returned.at[frm], rt_send.at[frm], rt_recv.at[frm], frm, g
+                result.at[b, frm], returned.at[b, frm], rt_send.at[b * 8 + frm],
+                rt_recv.at[b * 8 + frm], frm, g,
             ).wait_recv()
 
-        onehot_into(oh, hi_ref, ids_of(frm))
-        for b in range(8):
-            cells = slice(b * 512, (b + 1) * 512)
+        onehot_into(oh, hi_ref, half_ids(frm, b))
+        for part_of in range(8):
+            cells = slice(part_of * 512, (part_of + 1) * 512)
             total[:, cells] += lax.dot_general(
-                returned[frm], oh[cells, :], (((1,), (1,)), ((), ())), preferred_element_type=F32
+                returned[b, frm], oh[cells, 0:256], (((1,), (1,)), ((), ())),
+                preferred_element_type=F32,
             )
         return carry
 
-    lax.fori_loop(0, 8, place, 0)
+    lax.fori_loop(0, 16, place, 0)
     out_ref[...] = total[...].astype(BF16)
 
     for s in range(1, 8):
         z_copy(s).wait_send()
         state_copy((m + s) % 8).wait_send()
-        return_copy((m + s) % 8).wait_send()
+        for b in range(2):
+            return_copy((m + s) % 8, b).wait_send()
     param_sends(lambda sent: sent.wait_send())
     core_copy.wait_send()
     for r in range(9):
@@ -546,7 +576,7 @@
         in_specs=[vmem] * 5,
         out_specs=vmem,
         scratch_shapes=[
-            pltpu.VMEM((GROUPS, 4, POINTS), jnp.int32),
+            pltpu.VMEM((GROUPS, 2, 2, POINTS), jnp.int32),
             pltpu.VMEM((4, HEAD, POINTS), BF16),
             pltpu.VMEM((4, 2, HEAD, POINTS), BF16),
             pltpu.VMEM((2, 8, 2, HEAD, POINTS), BF16),
@@ -556,19 +586,20 @@
             pltpu.VMEM((8, ROWS, BLOCK), BF16),
             pltpu.VMEM((8, ROWS, BLOCK), BF16),
             pltpu.VMEM((FIELDS, BLOCK), F32),
-            pltpu.VMEM((MEMBERS * FIELDS, BLOCK), F32),
-            pltpu.VMEM((MEMBERS, GROUPS, 8, BLOCK), F32),
-            pltpu.VMEM((8, ROWS, BLOCK), BF16),
-            pltpu.VMEM((8, ROWS, BLOCK), BF16),
+            pltpu.VMEM((2, FIELDS, 256), F32),
+            pltpu.VMEM((2, MEMBERS * FIELDS, 256), F32),
+            pltpu.VMEM((2, MEMBERS, GROUPS, 8, 256), F32),
+            pltpu.VMEM((2, 8, ROWS, 256), BF16),
+            pltpu.VMEM((2, 8, ROWS, 256), BF16),
             pltpu.VMEM((ROWS, PATCH), F32),
             pltpu.VMEM((PATCH, BLOCK), BF16),
             pltpu.VMEM((64, BLOCK), F32),
             pltpu.VMEM((4, HEAD, POINTS), F32),
-            pltpu.VMEM((BLOCK, BLOCK), BF16),
-            pltpu.VMEM((4, POINTS, POINTS), BF16),
+            pltpu.VMEM((2, 256, 256), BF16),
+            pltpu.VMEM((2, POINTS, POINTS), BF16),
             dma((8,)), dma((8,)), dma((8,)), dma((8,)), dma((2,)), dma((1,)),
             dma((8,)), dma((18,)), dma((18,)), dma((18,)), dma((18,)), dma((18,)),
-            dma((8,)), dma((8,)), dma((8,)), dma((8,)),
+            dma((8,)), dma((8,)), dma((16,)), dma((16,)),
         ],
         compiler_params=pltpu.CompilerParams(
             collective_id=0, has_side_effects=True, vmem_limit_bytes=62 * 1024 * 1024

time: 85.1 us -> 77.7 us (0.913)
  the two profiles are of different devices: /device:TPU:34 before, /device:TPU:1 now
where the time goes in v4:
time: 77.7 us; the launch traced here: 77.4 us
  Pallas kernels  74.3 us (96%)
  local copies, waits for them, and re-layouts  3.02 us (4%)
    pallas_call x1, Pallas kernels, on_device(): pl.pallas_call(kernel, out_shape=jax.ShapeDtypeStruct((ROWS, PATCH), BF16...  74.3 us
    unnamed x1, local copies, waits for them, and re-layouts  3.02 us

profile of v4, /device:TPU:1, one launch (start us, length us, event | category | flops | bytes accessed | tf_op | source)
XLA Modules:
  0.0 77.4 jit_solution(14457288691618709782)
XLA Ops:
  0.0 74.3 %shard_map.55 = bf16[240,4096]{1,0:T(8,128)(2,1)} custom-call(bf16[240,4096]{1,0:T(8,128)(2,1)} %bitcast.6, s32[8,16,32]{2,1,0:T(8,128)} %bitcast.7, s32[3,1,512]{2,1,0:T(1,128)} %bitcast.8, f32[3,1,512]{2,1,0:T(1,128)} %bitcast.9, f32[1600,128]{1,0:T(8,128)} %trans_ref.1), custom_call_target="tpu_custom_call" | custom-call | tf_op jit(solution)/shard_map/pallas_call | solution.py:573
  74.3 3.0 %copy.7 = bf16[5,48,4096]{2,1,0:T(8,128)(2,1)} copy(bf16[5,48,4096]{2,1,0:T(8,128)(2,1)} %bitcast.5) | data formatting | bytes 3932160
